TPU v7x, 256 devices: a whole 4x4x8 slice. The times are simulated.
256 devices in a mesh: dp: 8 (over x, core), rows: 32 (over y, z).
Axes of the slice: x: 4, y: 4, z: 8, core: 2. Of those that a mesh axis runs over, the one named last changes fastest.
Arguments:
- grads: bfloat16 [2, 4096, 14336], P(None, 'rows', 'dp'), may hold values from -64 to 64
- basis: bfloat16 [2, 4096, 512], P(None, 'rows'), may hold values from -0.09375 to 0.09375
- moment1: float32 [2, 512, 14336], P(None, 'rows', 'dp'), may hold values from -0.3 to 0.3
- moment2: float32 [2, 512, 14336], P(None, 'rows', 'dp'), may hold values from 0.001 to 0.03
- weights: bfloat16 [2, 4096, 14336], P(None, 'rows', 'dp'), may hold values from -0.09375 to 0.09375
Outputs:
- new_weights: bfloat16 [2, 4096, 14336], P(None, 'rows')
- new_moment1: float32 [2, 512, 14336], P(None, 'rows', 'dp')
- new_moment2: float32 [2, 512, 14336], P(None, 'rows', 'dp')
All inputs are finite; a program needn't handle non-finite values.
Results may differ from a plain program's by a relative error of at most 0.00115.
The roundings to bfloat16 on the way count: a program that leaves them out, or rounds other values in their place, can miss the bound.
Values may be sent and summed in bfloat16 or wider, within the bound.
No kernel may reach another device: no remote copies, remote signals or barrier semaphores. Data moves between devices by JAX's collectives and lax.ppermute only.
A program may use at most 64 MiB of HBM per device.

v0:
```python
import math
import jax
import jax.numpy as jnp
from jax import lax
from jax.sharding import Mesh
from jax.sharding import PartitionSpec as P

D = 4096
FF = 14336
MATS = 2
STEP = 10
ROWS = ("rows_0", "rows_1")


def sum_by_axis(x, axes, dim):
    for axis in axes:
        x = lax.psum_scatter(x, axis, scatter_dimension=dim, tiled=True)
    return x


def laid_out(tiles, dim):
    tiles = jnp.moveaxis(tiles, 0, dim)
    shape = tiles.shape
    return tiles.reshape(*shape[:dim], shape[dim] * shape[dim + 1], *shape[dim + 2 :])


def gather_in_order(x, axes, turns):
    tiles = x[None]
    for k in turns:
        tiles = lax.all_gather(tiles, axes[k], axis=0, tiled=True)
    carried = [lax.axis_size(axes[k]) for k in reversed(turns)]
    tiles = tiles.reshape(*carried, *x.shape)
    turned = sorted(range(len(turns)), key=lambda place: turns[len(turns) - 1 - place])
    return tiles.transpose(*turned, *range(len(turns), tiles.ndim)).reshape(-1, *x.shape)


def whole_of(x, axes, turns, dim):
    return laid_out(gather_in_order(x, axes, turns), dim)


def moment_step(projected, moment1, moment2, total):
    limit = 1.0 * math.sqrt(MATS * D * FF)
    scale = limit / jnp.maximum(jnp.sqrt(total), limit)
    scaled = scale * projected
    first = 0.9 * moment1 + 0.1 * scaled
    second = 0.999 * moment2 + 0.001 * scaled * scaled
    first_bias_correction = 1.0 - 0.9**STEP
    second_fix = 1.0 - 0.999**STEP
    low_rank_update = (
        first / first_bias_correction / (jnp.sqrt(second / second_fix) + 1e-08)
    ).astype(jnp.bfloat16)
    return (first, second, low_rank_update)


def local(grads, basis, moment1, moment2, weights):
    grad_wide = grads.astype(jnp.float32)
    own_squares = jnp.sum(grad_wide * grad_wide)
    partial_norm_value = jnp.einsum(
        "yka,ykx->yax", basis, grads, preferred_element_type=jnp.float32
    )
    column_square_sum = jnp.full((lax.axis_size(ROWS),), own_squares, jnp.float32)
    projected, group_squares = (
        sum_by_axis(partial_norm_value, ROWS, 1),
        sum_by_axis(column_square_sum, ROWS, 0),
    )
    total = lax.psum(group_squares[0], "dp")
    first, second, low_rank_update = moment_step(projected, moment1, moment2, total)
    projected_back = jnp.einsum(
        "auw,awl->aul",
        basis,
        whole_of(low_rank_update, ROWS, (0, 1), 1),
        preferred_element_type=jnp.float32,
    )
    fresh = (weights.astype(jnp.float32) - 0.5 * projected_back).astype(jnp.bfloat16)
    whole_rows = lax.all_gather(fresh, "dp", axis=2, tiled=True)
    return (whole_rows, first, second)


def solution(mesh):
    finer = Mesh(mesh.devices.reshape(mesh.shape["dp"], 4, 8), ("dp", "rows_0", "rows_1"))
    in_specs = (
        P(None, ROWS, "dp"),
        P(None, ROWS, None),
        P(None, ROWS, "dp"),
        P(None, ROWS, "dp"),
        P(None, ROWS, "dp"),
    )
    out_specs = (P(None, ROWS, None), P(None, ROWS, "dp"), P(None, ROWS, "dp"))
    return jax.shard_map(local, mesh=finer, in_specs=in_specs, out_specs=out_specs, check_vma=False)
```

profile of v0, /device:TPU:1, one launch (start us, length us, event | category | flops | bytes accessed | tf_op | source)
XLA Modules:
  0.0 268.7 jit_solution(6423044746754964495)
XLA Ops:
  7.2 0.0 copy-start
  7.2 0.0 reduce-scatter.3.cloned.1.call-start
  7.2 0.9 copy-done
  8.1 5.4 %fusion.5 = f32[2,512,1792]{2,1,0:T(8,128)} fusion(bf16[2,128,512]{2,1,0:T(8,128)(2,1)S(1)} %copy-done, bf16[2,128,1792]{2,1,0:T(8,128)(2,1)} %param.5), kind=kOutput, calls=%fused_computation.9 | convolution fusion | flops 469762048 | bytes 8519680 | tf_op jit(solution)/shard_map/yka,ykx->yax/dot_general | solution.py:58
  13.5 0.0 copy-start.6
  13.5 0.0 copy-start.1
  13.5 0.0 copy-start.5
  13.5 0.0 copy-start.3
  13.5 0.0 copy-start.4
  13.5 0.0 reduce-scatter.3.cloned.1.call-update
  13.6 0.0 copy-start.2
  13.6 0.0 reduce-scatter.5.cloned.1.call-start
  13.6 78.9 %reduce-scatter.3.cloned.1.call-done = f32[2,128,1792]{2,1,0:T(8,128)} async-done(((f32[2,512,1792]{2,1,0:T(8,128)}), f32[2,128,1792]{2,1,0:T(8,128)}) %reduce-scatter.3.cloned.1.call-update) | async-done | bytes 1835024 | tf_op jit(solution)/shard_map/reduce_scatter | solution.py:17
  92.6 0.0 reduce-scatter.5.cloned.1.call-update
  92.6 0.0 all-gather.4.cloned.1.call-start
  92.6 0.0 copy-done.6
  92.6 0.6 dynamic-slice
  93.9 0.0 copy-done.1
  93.9 1.1 multiply_reduce_fusion
  95.0 0.6 broadcast_in_dim.6
  95.6 6.6 %all-reduce = f32[32]{0:T(128)S(1)} all-reduce(f32[32]{0:T(128)S(1)} %broadcast_in_dim.6), channel_id=3, replica_groups=mesh['dp'=8,'rows_0'=4,'rows_1'=8] {'rows_0'}, use_global_device_ids=true, to_apply=%region_1.0.clone | all-reduce | flops 32 | bytes 256
  102.2 0.1 dynamic-slice.1
  102.2 14.4 %all-reduce.1 = f32[8]{0:T(128)S(1)} all-reduce(f32[8]{0:T(128)S(1)} %dynamic-slice.1), channel_id=4, replica_groups=mesh['dp'=8,'rows_0'=4,'rows_1'=8] {'rows_1'}, use_global_device_ids=true, to_apply=%region_2.0.clone | all-reduce | flops 8 | bytes 64
  116.6 0.0 copy-done.5
  116.6 0.6 dynamic-slice.2
  117.2 1.2 dynamic-slice.3
  118.5 18.6 %psum.7 = f32[]{:T(128)} all-reduce(f32[]{:T(128)} %bitcast), channel_id=1, replica_groups=mesh['dp'=8,'rows_0'=4,'rows_1'=8] {'dp'}, use_global_device_ids=true, to_apply=%region_3.0 | all-reduce | flops 1 | bytes 8 | tf_op jit(solution)/shard_map/psum | solution.py:66
  137.8 0.0 reduce-scatter.5.cloned.1.call-done
  137.9 0.0 copy-done.3
  137.9 0.0 copy-done.4
  137.9 1.8 divide_convert_fusion
  139.7 10.5 %all-gather = bf16[8,16,1792]{2,1,0:T(8,128)(2,1)} all-gather(bf16[2,16,1792]{2,1,0:T(8,128)(2,1)S(1)} %get-tuple-element.12), channel_id=2, replica_groups=mesh['dp'=8,'rows_0'=4,'rows_1'=8] {'rows_0'}, dimensions={0}, use_global_device_ids=true | all-gather | bytes 573440 | tf_op jit(solution)/shard_map/all_gather | solution.py:30
  150.2 0.0 all-gather.4.cloned.1.call-update
  150.2 0.0 all-gather.6.cloned.1.call-start
  150.3 0.0 copy-done.2
  150.3 0.6 copy.17
  150.9 49.1 %all-gather.4.cloned.1.call-done = bf16[32,2,16,1792]{3,2,1,0:T(8,128)(2,1)} async-done(((bf16[4,2,16,1792]{3,2,1,0:T(8,128)(2,1)}), bf16[32,2,16,1792]{3,2,1,0:T(8,128)(2,1)}) %all-gather.4.cloned.1.call-update) | async-done | bytes 3670032 | tf_op jit(solution)/shard_map/all_gather | solution.py:30
  200.0 2.3 copy.19
  202.4 2.5 fusion.2
  204.9 0.0 all-gather.6.cloned.1.call-update
  204.9 47.1 %all-gather.6.cloned.1.call-done = bf16[2,128,14336]{1,2,0:T(8,128)(2,1)} async-done(((bf16[2,128,1792]{1,2,0:T(8,128)(2,1)}), bf16[2,128,14336]{1,2,0:T(8,128)(2,1)}) %all-gather.6.cloned.1.call-update) | async-done | bytes 7340048 | tf_op jit(solution)/shard_map/all_gather | solution.py:75
  252.0 10.1 %copy.21 = bf16[2,128,14336]{2,1,0:T(8,128)(2,1)} copy(bf16[2,128,14336]{1,2,0:T(8,128)(2,1)} %all-gather.6.cloned.1.call-done) | data formatting | bytes 14680064
Async XLA Ops:
  7.2 1.0 copy-start
  7.2 85.4 %reduce-scatter.3.cloned.1.call-start = ((), (), s32[]{:S(2)}) async-start(), calls=%async_computation.2 | async-start | bytes 9175040 | tf_op jit(solution)/shard_map/reduce_scatter | solution.py:17
  13.5 79.1 %copy-start.6 = (u32[256]{0:T(256)S(1)}, u32[256]{0:T(256)}, u32[]{:S(2)}) copy-start(u32[256]{0:T(256)} %constant.26) | copy-start | bytes 3076
  13.5 80.4 %copy-start.1 = (bf16[2,128,1792]{2,1,0:T(8,128)(2,1)S(1)}, bf16[2,128,1792]{2,1,0:T(8,128)(2,1)}, u32[]{:S(2)}) copy-start(bf16[2,128,1792]{2,1,0:T(8,128)(2,1)} %param.5) | copy-start | bytes 2752516
  13.5 103.1 %copy-start.5 = (u32[256]{0:T(256)S(1)}, u32[256]{0:T(256)}, u32[]{:S(2)}) copy-start(u32[256]{0:T(256)} %constant.30) | copy-start | bytes 3076
  13.5 124.3 %copy-start.3 = (f32[2,16,1792]{2,1,0:T(8,128)S(1)}, f32[2,16,1792]{2,1,0:T(8,128)}, u32[]{:S(2)}) copy-start(f32[2,16,1792]{2,1,0:T(8,128)} %param.7) | copy-start | bytes 688132
  13.5 124.4 %copy-start.4 = (f32[2,16,1792]{2,1,0:T(8,128)S(1)}, f32[2,16,1792]{2,1,0:T(8,128)}, u32[]{:S(2)}) copy-start(f32[2,16,1792]{2,1,0:T(8,128)} %param.8) | copy-start | bytes 688132
  13.6 136.7 %copy-start.2 = (bf16[2,128,1792]{2,1,0:T(8,128)(2,1)S(1)}, bf16[2,128,1792]{2,1,0:T(8,128)(2,1)}, u32[]{:S(2)}) copy-start(bf16[2,128,1792]{2,1,0:T(8,128)(2,1)} %param.9) | copy-start | bytes 2752516
  13.6 124.3 %reduce-scatter.5.cloned.1.call-start = ((), (), s32[]{:S(2)}) async-start(), calls=%async_computation.3 | async-start | bytes 2064384 | tf_op jit(solution)/shard_map/reduce_scatter | solution.py:17
  92.6 107.5 %all-gather.4.cloned.1.call-start = ((), (), s32[]{:S(2)}) async-start(), calls=%async_computation.4 | async-start | bytes 4128768 | tf_op jit(solution)/shard_map/all_gather | solution.py:30
  150.2 101.8 %all-gather.6.cloned.1.call-start = ((), (), s32[]{:S(2)}) async-start(), calls=%async_computation.5 | async-start | bytes 8257536 | tf_op jit(solution)/shard_map/all_gather | solution.py:75
Sparse Core Ops, SparseCore 0:
  13.7 78.8 reduce-scatter.2
  95.1 37.1 reduce-scatter.4
  150.4 49.6 all-gather.3
  205.0 46.9 all-gather.5
where the time goes:
time: 269 us
  waiting for transfers between devices  175 us (65%)
  blocking collectives  50.1 us (19%)
  local copies, waits for them, and re-layouts  17.1 us (6%)
  between operations  15.3 us (6%)
  matrix products  7.89 us (3%)
  other arithmetic  2.92 us (1%)
    reduce_scatter x2, waiting for transfers between devices, sum_by_axis(): x = lax.psum_scatter(x, axis, scatter_dimension=dim, tiled=True)  79 us
    all_gather x1, waiting for transfers between devices, gather_in_order(): tiles = lax.all_gather(tiles, axes[k], axis=0, tiled=True)  49.1 us
    all_gather x1, waiting for transfers between devices, local(): whole_rows = lax.all_gather(fresh, 'dp', axis=2, tiled=True)  47.1 us
    unnamed x2, blocking collectives  20.9 us
    psum x1, blocking collectives, local(): total = lax.psum(group_squares[0], 'dp')  18.6 us
    unnamed x20, local copies, waits for them, and re-layouts  14.2 us
    all_gather x1, blocking collectives, gather_in_order(): tiles = lax.all_gather(tiles, axes[k], axis=0, tiled=True)  10.5 us
    dot_general x1, matrix products, local(): jnp.einsum('yka,ykx->yax', basis, grads, preferred_element_type=jnp.float32)  5.38 us
  transfers between devices with their start and end apart: 4, of which 3 were waited for; matrix products, arithmetic and copies ran while one was open for 2% of the time, Pallas kernels for 0%

commit v1 on v0

--- a/solution.py
+++ b/solution.py
@@ -72,7 +72,8 @@
         preferred_element_type=jnp.float32,
     )
     fresh = (weights.astype(jnp.float32) - 0.5 * projected_back).astype(jnp.bfloat16)
-    whole_rows = lax.all_gather(fresh, "dp", axis=2, tiled=True)
+    sent = jnp.stack([fresh] * lax.axis_size("dp"))
+    whole_rows = jnp.concatenate(lax.all_to_all(sent, "dp", 0, 0), axis=2)
     return (whole_rows, first, second)
 
 

time: 269 us -> 320 us (1.19)
  blocking collectives: 50.1 us -> 137 us
  waiting for transfers between devices: 175 us -> 128 us
  local copies, waits for them, and re-layouts: 17.1 us -> 28.4 us
    all_to_all x0 -> x1, blocking collectives: none -> 87.3 us  [local(): whole_rows = jnp.concatenate(lax.all_to_all(sent, 'dp', 0, 0), axis=2)]
    all_gather x1 -> x0, waiting for transfers between devices: 47.1 us -> none  [local(): whole_rows = lax.all_gather(fresh, 'dp', axis=2, tiled=True)]
    all_to_all x0 -> x1, local copies, waits for them, and re-layouts: none -> 10 us  [local(): whole_rows = jnp.concatenate(lax.all_to_all(sent, 'dp', 0, 0), axis=2)]
  transfers between devices with their start and end apart: 4 -> 3, of which waited for: 3 -> 2; matrix products, arithmetic and copies ran while one was open for 2% -> 2% of each run, Pallas kernels for 0% -> 0%
where the time goes in v1:
time: 320 us; the launch traced here: 319 us
  blocking collectives  137 us (43%)
  waiting for transfers between devices  128 us (40%)
  local copies, waits for them, and re-layouts  28.4 us (9%)
  between operations  15.3 us (5%)
  matrix products  6.96 us (2%)
    all_to_all x1, blocking collectives, local(): whole_rows = jnp.concatenate(lax.all_to_all(sent, 'dp', 0, 0), axis=2)  87.3 us
    reduce_scatter x2, waiting for transfers between devices, sum_by_axis(): x = lax.psum_scatter(x, axis, scatter_dimension=dim, tiled=True)  79 us
    all_gather x1, waiting for transfers between devices, gather_in_order(): tiles = lax.all_gather(tiles, axes[k], axis=0, tiled=True)  49.2 us
    unnamed x2, blocking collectives  20.9 us
    psum x1, blocking collectives, local(): total = lax.psum(group_squares[0], 'dp')  18.6 us
    unnamed x20, local copies, waits for them, and re-layouts  14.2 us
    all_gather x1, blocking collectives, gather_in_order(): tiles = lax.all_gather(tiles, axes[k], axis=0, tiled=True)  10.5 us
    all_to_all x1, local copies, waits for them, and re-layouts, local(): whole_rows = jnp.concatenate(lax.all_to_all(sent, 'dp', 0, 0), axis=2)  10 us
  transfers between devices with their start and end apart: 3, of which 2 were waited for; matrix products, arithmetic and copies ran while one was open for 2% of the time, Pallas kernels for 0%

profile of v1, /device:TPU:1, one launch (start us, length us, event | category | flops | bytes accessed | tf_op | source)
XLA Modules:
  0.0 319.3 jit_solution(3272971600563607807)
XLA Ops:
  7.2 0.0 copy-start
  7.2 0.0 reduce-scatter.3.cloned.1.call-start
  7.2 0.9 copy-done
  8.1 5.4 %fusion.5 = f32[2,512,1792]{2,1,0:T(8,128)} fusion(bf16[2,128,512]{2,1,0:T(8,128)(2,1)S(1)} %copy-done, bf16[2,128,1792]{2,1,0:T(8,128)(2,1)} %param.5), kind=kOutput, calls=%fused_computation.9 | convolution fusion | flops 469762048 | bytes 8519680 | tf_op jit(solution)/shard_map/yka,ykx->yax/dot_general | solution.py:58
  13.5 0.0 copy-start.6
  13.5 0.0 copy-start.1
  13.5 0.0 copy-start.5
  13.5 0.0 copy-start.3
  13.5 0.0 copy-start.4
  13.5 0.0 reduce-scatter.3.cloned.1.call-update
  13.6 0.0 copy-start.2
  13.6 0.0 reduce-scatter.5.cloned.1.call-start
  13.6 78.9 %reduce-scatter.3.cloned.1.call-done = f32[2,128,1792]{2,1,0:T(8,128)} async-done(((f32[2,512,1792]{2,1,0:T(8,128)}), f32[2,128,1792]{2,1,0:T(8,128)}) %reduce-scatter.3.cloned.1.call-update) | async-done | bytes 1835024 | tf_op jit(solution)/shard_map/reduce_scatter | solution.py:17
  92.6 0.0 reduce-scatter.5.cloned.1.call-update
  92.6 0.0 all-gather.3.cloned.1.call-start
  92.6 0.0 copy-done.6
  92.6 0.6 dynamic-slice
  93.9 0.0 copy-done.1
  93.9 1.1 multiply_reduce_fusion
  95.0 0.6 broadcast_in_dim.6
  95.6 6.6 %all-reduce = f32[32]{0:T(128)S(1)} all-reduce(f32[32]{0:T(128)S(1)} %broadcast_in_dim.6), channel_id=3, replica_groups=mesh['dp'=8,'rows_0'=4,'rows_1'=8] {'rows_0'}, use_global_device_ids=true, to_apply=%region_1.0.clone | all-reduce | flops 32 | bytes 256
  102.2 0.1 dynamic-slice.1
  102.2 14.4 %all-reduce.1 = f32[8]{0:T(128)S(1)} all-reduce(f32[8]{0:T(128)S(1)} %dynamic-slice.1), channel_id=4, replica_groups=mesh['dp'=8,'rows_0'=4,'rows_1'=8] {'rows_1'}, use_global_device_ids=true, to_apply=%region_2.0.clone | all-reduce | flops 8 | bytes 64
  116.6 0.0 copy-done.5
  116.6 0.6 dynamic-slice.2
  117.2 1.2 dynamic-slice.3
  118.5 18.6 %psum.7 = f32[]{:T(128)} all-reduce(f32[]{:T(128)} %bitcast), channel_id=1, replica_groups=mesh['dp'=8,'rows_0'=4,'rows_1'=8] {'dp'}, use_global_device_ids=true, to_apply=%region_3.0 | all-reduce | flops 1 | bytes 8 | tf_op jit(solution)/shard_map/psum | solution.py:66
  137.8 0.0 reduce-scatter.5.cloned.1.call-done
  137.9 0.0 copy-done.3
  137.9 0.0 copy-done.4
  137.9 1.8 divide_convert_fusion
  139.7 10.5 %all-gather = bf16[8,16,1792]{2,1,0:T(8,128)(2,1)} all-gather(bf16[2,16,1792]{2,1,0:T(8,128)(2,1)S(1)} %get-tuple-element.6), channel_id=2, replica_groups=mesh['dp'=8,'rows_0'=4,'rows_1'=8] {'rows_0'}, dimensions={0}, use_global_device_ids=true | all-gather | bytes 573440 | tf_op jit(solution)/shard_map/all_gather | solution.py:30
  150.2 0.0 all-gather.3.cloned.1.call-update
  150.2 0.0 copy-done.2
  150.3 0.6 copy.22
  150.9 49.2 %all-gather.3.cloned.1.call-done = bf16[32,2,16,1792]{3,2,1,0:T(8,128)(2,1)} async-done(((bf16[4,2,16,1792]{3,2,1,0:T(8,128)(2,1)}), bf16[32,2,16,1792]{3,2,1,0:T(8,128)(2,1)}) %all-gather.3.cloned.1.call-update) | async-done | bytes 3670032 | tf_op jit(solution)/shard_map/all_gather | solution.py:30
  200.0 2.3 copy.24
  202.4 1.6 fusion.2
  204.0 0.5 copy.26
  204.5 0.7 stack.2
  205.2 87.3 %all_to_all.5 = bf16[8,2,128,1792]{3,2,1,0:T(8,128)(2,1)} all-to-all(bf16[8,2,128,1792]{3,2,1,0:T(8,128)(2,1)S(1)} %stack.2), channel_id=1, replica_groups=mesh['dp'=8,'rows_0'=4,'rows_1'=8] {'dp'}, dimensions={0} | all-to-all | bytes 14680064 | tf_op jit(solution)/shard_map/all_to_all | solution.py:76
  292.6 10.0 %copy.27 = bf16[8,2,128,1792]{2,3,0,1:T(8,128)(2,1)} copy(bf16[8,2,128,1792]{3,2,1,0:T(8,128)(2,1)} %all_to_all.5) | data formatting | bytes 14680064 | tf_op jit(solution)/shard_map/all_to_all | solution.py:76
  302.6 10.1 %copy.28 = bf16[2,128,14336]{2,1,0:T(8,128)(2,1)} copy(bf16[2,128,14336]{1,2,0:T(8,128)(2,1)} %bitcast.25) | data formatting | bytes 14680064
Async XLA Ops:
  7.2 1.0 copy-start
  7.2 85.4 %reduce-scatter.3.cloned.1.call-start = ((), (), s32[]{:S(2)}) async-start(), calls=%async_computation.3 | async-start | bytes 9175040 | tf_op jit(solution)/shard_map/reduce_scatter | solution.py:17
  13.5 79.1 %copy-start.6 = (u32[256]{0:T(256)S(1)}, u32[256]{0:T(256)}, u32[]{:S(2)}) copy-start(u32[256]{0:T(256)} %constant.26) | copy-start | bytes 3076
  13.5 80.4 %copy-start.1 = (bf16[2,128,1792]{2,1,0:T(8,128)(2,1)S(1)}, bf16[2,128,1792]{2,1,0:T(8,128)(2,1)}, u32[]{:S(2)}) copy-start(bf16[2,128,1792]{2,1,0:T(8,128)(2,1)} %param.5) | copy-start | bytes 2752516
  13.5 103.1 %copy-start.5 = (u32[256]{0:T(256)S(1)}, u32[256]{0:T(256)}, u32[]{:S(2)}) copy-start(u32[256]{0:T(256)} %constant.30) | copy-start | bytes 3076
  13.5 124.3 %copy-start.3 = (f32[2,16,1792]{2,1,0:T(8,128)S(1)}, f32[2,16,1792]{2,1,0:T(8,128)}, u32[]{:S(2)}) copy-start(f32[2,16,1792]{2,1,0:T(8,128)} %param.7) | copy-start | bytes 688132
  13.5 124.4 %copy-start.4 = (f32[2,16,1792]{2,1,0:T(8,128)S(1)}, f32[2,16,1792]{2,1,0:T(8,128)}, u32[]{:S(2)}) copy-start(f32[2,16,1792]{2,1,0:T(8,128)} %param.8) | copy-start | bytes 688132
  13.6 136.7 %copy-start.2 = (bf16[2,128,1792]{2,1,0:T(8,128)(2,1)S(1)}, bf16[2,128,1792]{2,1,0:T(8,128)(2,1)}, u32[]{:S(2)}) copy-start(bf16[2,128,1792]{2,1,0:T(8,128)(2,1)} %param.9) | copy-start | bytes 2752516
  13.6 124.3 %reduce-scatter.5.cloned.1.call-start = ((), (), s32[]{:S(2)}) async-start(), calls=%async_computation.4 | async-start | bytes 2064384 | tf_op jit(solution)/shard_map/reduce_scatter | solution.py:17
  92.6 107.5 %all-gather.3.cloned.1.call-start = ((), (), s32[]{:S(2)}) async-start(), calls=%async_computation.5 | async-start | bytes 4128768 | tf_op jit(solution)/shard_map/all_gather | solution.py:30
Sparse Core Ops, SparseCore 0:
  13.7 78.8 reduce-scatter.2
  95.1 37.1 reduce-scatter.4
  150.4 49.6 all-gather.2
